TPU v7x, 32 devices: a whole 2x2x4 slice. The times are simulated.
32 devices in a mesh: ia: 4 (over z), ja: 2 (over core), ka: 4 (over y, x).
Axes of the slice: x: 2, y: 2, z: 4, core: 2. Of those that a mesh axis runs over, the one named last changes fastest.
Arguments:
- attended: bfloat16 [1024, 8192], P('ia', ('ja', 'ka')), may hold values from -6 to 6
- out_weight: bfloat16 [8192, 8192], P(('ja', 'ia'), 'ka'), may hold values from -0.0625 to 0.0625
- cotangent: bfloat16 [1024, 8192], P('ia', ('ka', 'ja')), may hold values from -3 to 3
Outputs:
- projected: bfloat16 [1024, 8192], P('ia', ('ka', 'ja'))
- input_grad: bfloat16 [1024, 8192], P('ia', ('ja', 'ka'))
- weight_grad: bfloat16 [8192, 8192], P(('ja', 'ia'), 'ka')
All inputs are finite; a program needn't handle non-finite values.
Results may differ from a plain program's by a relative error of at most 0.015.
Values may be sent and summed in bfloat16 or wider, within the bound.
A program may use at most 128 MiB of HBM per device.

v0:
```python
import jax
import jax.numpy as jnp
from jax import lax
from jax.sharding import PartitionSpec as P


def on_device(attended, out_weight, cotangent):
    head_rows = lax.all_gather(attended, "ka", axis=1, tiled=True)
    weight_local = lax.all_gather(out_weight, "ia", axis=0, tiled=True)
    partial_value = jnp.dot(head_rows, weight_local, preferred_element_type=jnp.float32)
    projected = (
        lax.psum_scatter(partial_value.astype(jnp.bfloat16), "ja", scatter_dimension=1, tiled=True)
        .astype(jnp.float32)
        .astype(jnp.bfloat16)
    )
    grad_rows = lax.all_gather(cotangent, "ja", axis=1, tiled=True)
    input_terms = lax.dot_general(
        grad_rows, weight_local, (((1,), (1,)), ((), ())), preferred_element_type=jnp.float32
    )
    input_grad = (
        lax.psum_scatter(input_terms.astype(jnp.bfloat16), "ka", scatter_dimension=1, tiled=True)
        .astype(jnp.float32)
        .astype(jnp.bfloat16)
    )
    weight_terms = lax.dot_general(
        head_rows, grad_rows, (((0,), (0,)), ((), ())), preferred_element_type=jnp.float32
    )
    weight_grad = lax.psum_scatter(
        weight_terms.astype(jnp.bfloat16), "ia", scatter_dimension=0, tiled=True
    ).astype(jnp.float32)
    return (projected, input_grad, weight_grad.astype(jnp.bfloat16))


def solution(mesh):
    return jax.shard_map(
        on_device,
        mesh=mesh,
        in_specs=(P("ia", ("ja", "ka")), P(("ja", "ia"), "ka"), P("ia", ("ka", "ja"))),
        out_specs=(P("ia", ("ka", "ja")), P("ia", ("ja", "ka")), P(("ja", "ia"), "ka")),
        check_vma=False,
    )
```

profile of v0, /device:TPU:8, one launch (start us, length us, event | category | flops | bytes accessed | tf_op | source)
XLA Modules:
  0.0 683.2 jit_solution(17482856159196873137)
XLA Ops:
  7.2 0.0 all-gather.4.cloned.1.call-start
  7.2 0.7 all-gather.4.cloned.1.call-update
  7.9 0.0 all-gather.6.cloned.1.call-start
  7.9 0.7 all-gather.6.cloned.1.call-update
  8.6 0.0 all-gather.8.cloned.1.call-start
  8.7 0.7 all-gather.8.cloned.1.call-update
  9.4 0.0 reduce-scatter.4.cloned.1.call-start
  9.4 36.5 %all-gather.4.cloned.1.call-done = bf16[256,4096]{1,0:T(8,128)(2,1)} async-done(((bf16[256,1024]{1,0:T(8,128)(2,1)}), bf16[256,4096]{1,0:T(8,128)(2,1)}) %all-gather.4.cloned.1.call-update) | async-done | bytes 2097168 | tf_op jit(solution)/shard_map/all_gather | solution.py:8
  46.0 285.2 %all-gather.6.cloned.1.call-done = bf16[4096,2048]{1,0:T(8,128)(2,1)} async-done(((bf16[1024,2048]{1,0:T(8,128)(2,1)}), bf16[4096,2048]{1,0:T(8,128)(2,1)}) %all-gather.6.cloned.1.call-update) | async-done | bytes 16777232 | tf_op jit(solution)/shard_map/all_gather | solution.py:9
  331.2 11.9 %convolution_convert_fusion.2 = bf16[256,2048]{1,0:T(8,128)(2,1)} fusion(bf16[256,4096]{1,0:T(8,128)(2,1)} %all-gather.4.cloned.1.call-done, bf16[4096,2048]{1,0:T(8,128)(2,1)} %all-gather.6.cloned.1.call-done), kind=kOutput, calls=%fused_computation.2 | convolution fusion | flops 4295491584 | bytes 19922944 | tf_op jit(solution)/shard_map/dot_general | solution.py:10
  343.1 0.0 reduce-scatter.4.cloned.1.call-update
  343.1 0.0 copy-start
  343.1 0.0 reduce-scatter.6.cloned.1.call-start
  343.1 0.1 all-gather.8.cloned.1.call-done
  343.2 0.0 copy-start.1
  343.2 12.1 %convolution_convert_fusion.1 = bf16[256,4096]{1,0:T(8,128)(2,1)} fusion(bf16[256,2048]{1,0:T(8,128)(2,1)} %all-gather.8.cloned.1.call-done, bf16[4096,2048]{1,0:T(8,128)(2,1)} %all-gather.6.cloned.1.call-done), kind=kOutput, calls=%fused_computation.1 | convolution fusion | flops 4296015872 | bytes 19922944 | tf_op jit(solution)/shard_map/dot_general | solution.py:17
  355.3 0.0 reduce-scatter.6.cloned.1.call-update
  355.3 0.0 reduce-scatter.8.cloned.1.call-start
  355.4 0.0 copy-done
  355.4 0.0 copy-done.1
  355.4 8.2 %convolution_convert_fusion = bf16[4096,2048]{1,0:T(8,128)(2,1)} fusion(bf16[256,4096]{1,0:T(8,128)(2,1)S(1)} %copy-done, bf16[256,2048]{1,0:T(8,128)(2,1)S(1)} %copy-done.1), kind=kOutput, calls=%fused_computation | convolution fusion | flops 4303355904 | bytes 19922944 | tf_op jit(solution)/shard_map/dot_general | solution.py:25
  363.5 0.0 reduce-scatter.8.cloned.1.call-update
  363.6 0.0 reduce-scatter.4.cloned.1.call-done
  363.6 31.2 %reduce-scatter.6.cloned.1.call-done = bf16[256,1024]{1,0:T(8,128)(2,1)} async-done(((bf16[256,4096]{1,0:T(8,128)(2,1)}), bf16[256,1024]{1,0:T(8,128)(2,1)}) %reduce-scatter.6.cloned.1.call-update) | async-done | bytes 524304 | tf_op jit(solution)/shard_map/reduce_scatter | solution.py:21
  394.7 281.6 %reduce-scatter.8.cloned.1.call-done = bf16[1024,2048]{1,0:T(8,128)(2,1)} async-done(((bf16[4096,2048]{1,0:T(8,128)(2,1)}), bf16[1024,2048]{1,0:T(8,128)(2,1)}) %reduce-scatter.8.cloned.1.call-update) | async-done | bytes 4194320 | tf_op jit(solution)/shard_map/reduce_scatter | solution.py:28
Async XLA Ops:
  7.2 38.8 %all-gather.4.cloned.1.call-start = ((), (), s32[]{:S(2)}) async-start(), calls=%async_computation.3 | async-start | bytes 2621440 | tf_op jit(solution)/shard_map/all_gather | solution.py:8
  7.9 323.3 %all-gather.6.cloned.1.call-start = ((), (), s32[]{:S(2)}) async-start(), calls=%async_computation.4 | async-start | bytes 20971520 | tf_op jit(solution)/shard_map/all_gather | solution.py:9
  8.6 334.6 %all-gather.8.cloned.1.call-start = ((), (), s32[]{:S(2)}) async-start(), calls=%async_computation.6 | async-start | bytes 1572864 | tf_op jit(solution)/shard_map/all_gather | solution.py:16
  9.4 354.2 %reduce-scatter.4.cloned.1.call-start = ((), (), s32[]{:S(2)}) async-start(), calls=%async_computation.5 | async-start | bytes 1572864 | tf_op jit(solution)/shard_map/reduce_scatter | solution.py:12
  343.1 12.3 %copy-start = (bf16[256,4096]{1,0:T(8,128)(2,1)S(1)}, bf16[256,4096]{1,0:T(8,128)(2,1)}, u32[]{:S(2)}) copy-start(bf16[256,4096]{1,0:T(8,128)(2,1)} %all-gather.4.cloned.1.call-done) | copy-start | bytes 6291460
  343.1 51.7 %reduce-scatter.6.cloned.1.call-start = ((), (), s32[]{:S(2)}) async-start(), calls=%async_computation.7 | async-start | bytes 2621440 | tf_op jit(solution)/shard_map/reduce_scatter | solution.py:21
  343.2 12.2 %copy-start.1 = (bf16[256,2048]{1,0:T(8,128)(2,1)S(1)}, bf16[256,2048]{1,0:T(8,128)(2,1)}, u32[]{:S(2)}) copy-start(bf16[256,2048]{1,0:T(8,128)(2,1)} %all-gather.8.cloned.1.call-done) | copy-start | bytes 3145732
  355.3 321.1 %reduce-scatter.8.cloned.1.call-start = ((), (), s32[]{:S(2)}) async-start(), calls=%async_computation.8 | async-start | bytes 20971520 | tf_op jit(solution)/shard_map/reduce_scatter | solution.py:28
Sparse Core Ops, SparseCore 0:
  9.8 36.1 all-gather.3
  47.5 283.6 all-gather.5
  332.7 10.4 all-gather.7
  345.9 9.5 reduce-scatter.3
  358.8 35.8 reduce-scatter.5
  397.5 278.7 reduce-scatter.7
where the time goes:
time: 685 us; the launch traced here: 683 us
  waiting for transfers between devices  637 us (93%)
  matrix products  32.1 us (5%)
  between operations  14.1 us (2%)
    all_gather x1, waiting for transfers between devices, on_device(): weight_local = lax.all_gather(out_weight, 'ia', axis=0, tiled=True)  285 us
    reduce_scatter x1, waiting for transfers between devices, on_device(): lax.psum_scatter(weight_terms.astype(jnp.bfloat16), 'ia', scatter_dimensi...  282 us
    all_gather x1, waiting for transfers between devices, on_device(): head_rows = lax.all_gather(attended, 'ka', axis=1, tiled=True)  36.5 us
    reduce_scatter x1, waiting for transfers between devices, on_device(): lax.psum_scatter(input_terms.astype(jnp.bfloat16), 'ka', scatter_dimensio...  31.2 us
  transfers between devices with their start and end apart: 6, of which 5 were waited for; matrix products, arithmetic and copies ran while one was open for 5% of the time, Pallas kernels for 0%

commit v1 on v0

v1 whole, which is shorter than its diff:
```python
import functools

import jax
import jax.numpy as jnp
from jax import lax
from jax.experimental import pallas as pl
from jax.experimental.pallas import tpu as pltpu
from jax.sharding import PartitionSpec as P

MESH = pl.DeviceIdType.MESH
VMEM_LIMIT = 60 * 1024 * 1024


def gathered_weight(attended, out_weight, cotangent):
    head_rows = lax.all_gather(attended, "ka", axis=1, tiled=True)
    weight_local = lax.all_gather(out_weight, "ia", axis=0, tiled=True)
    partial_value = jnp.dot(head_rows, weight_local, preferred_element_type=jnp.float32)
    projected = lax.psum_scatter(
        partial_value.astype(jnp.bfloat16), "ja", scatter_dimension=1, tiled=True
    )
    grad_rows = lax.all_gather(cotangent, "ja", axis=1, tiled=True)
    input_terms = lax.dot_general(
        grad_rows, weight_local, (((1,), (1,)), ((), ())), preferred_element_type=jnp.float32
    )
    input_grad = lax.psum_scatter(
        input_terms.astype(jnp.bfloat16), "ka", scatter_dimension=1, tiled=True
    )
    weight_terms = lax.dot_general(
        head_rows, grad_rows, (((0,), (0,)), ((), ())), preferred_element_type=jnp.float32
    )
    weight_grad = lax.psum_scatter(
        weight_terms.astype(jnp.bfloat16), "ia", scatter_dimension=0, tiled=True
    )
    return projected, input_grad, weight_grad


def kernel(
    n, att, w_hbm, cot, proj, ig, wg,
    w, a_x, a_g, c_g, p_send, p_recv, p_own, z_buf, z_up, z_dn,
    i_part, i_recv, i_red, i_z, i_out,
    loc, sa, ra, sb, rb_, sc, rc, su, ru, sd, rd, spu, rpu, spd, rpd, spo, rpo,
    sp, rp, sru, rru, srd, rrd, si, ri, sz, rz, so, ro,
):
    ia, ja, ka = lax.axis_index("ia"), lax.axis_index("ja"), lax.axis_index("ka")
    other = 1 - ja
    tok, head = att.shape
    quart = tok // n
    half = cot.shape[1]
    rows_w = w.shape[0]
    f32, bf16 = jnp.float32, jnp.bfloat16

    def plus(x, r):
        return lax.rem(x + r, n)

    def minus(x, r):
        return lax.rem(x + n - r, n)

    def span(t):
        return pl.ds(pl.multiple_of(t * tok, tok), tok)

    def piece(t, q):
        return pl.ds(pl.multiple_of(t * tok + q * quart, quart), quart)

    def remote(src, dst, s, r, where):
        return pltpu.make_async_remote_copy(
            src_ref=src, dst_ref=dst, send_sem=s, recv_sem=r,
            device_id=where, device_id_type=MESH,
        )

    barrier = pltpu.get_barrier_semaphore()
    for r in range(1, n):
        pl.semaphore_signal(barrier, inc=1, device_id={"ka": plus(ka, r)}, device_id_type=MESH)
        pl.semaphore_signal(barrier, inc=1, device_id={"ia": plus(ia, r)}, device_id_type=MESH)
    pl.semaphore_signal(barrier, inc=1, device_id={"ja": other}, device_id_type=MESH)
    pl.semaphore_wait(barrier, 2 * (n - 1) + 1)

    def a_plane(r):
        q = plus(ka, r)
        return remote(att.at[pl.ds(pl.multiple_of(q * quart, quart), quart)], a_x.at[ka],
                      sa.at[r - 1], ra.at[r - 1], {"ka": q})

    def a_z(r):
        z = plus(ia, r)
        return remote(a_x.at[z], a_g.at[piece(ia, ka)], sb.at[r - 1], rb_.at[r - 1], {"ia": z})

    def a_spread(b, r):
        rows = a_g.at[piece(minus(ia, b), ka)]
        return remote(rows, rows, sc.at[b, r - 1], rc.at[b, r - 1], {"ka": plus(ka, r)})

    def c_up(d):
        block = c_g.at[ja, span(ia - (d - 1))]
        src = cot if d == 1 else block
        return remote(src, block, su.at[d - 1], ru.at[d - 1], {"ia": ia + 1})

    def c_down(d):
        block = c_g.at[ja, span(ia + (d - 1))]
        src = cot if d == 1 else block
        return remote(src, block, sd.at[d - 1], rd.at[d - 1], {"ia": ia - 1})

    def c_pair_up(d):
        block = c_g.at[ja, span(ia - d)]
        return remote(block, block, spu.at[d - 1], rpu.at[d - 1], {"ja": other})

    def c_pair_down(d):
        block = c_g.at[ja, span(ia + d)]
        return remote(block, block, spd.at[d - 1], rpd.at[d - 1], {"ja": other})

    c_pair_own = remote(cot, c_g.at[ja, span(ia)], spo.at[0], rpo.at[0], {"ja": other})

    def up_exists(d):
        return jnp.logical_and(ia + 1 < n, ia - (d - 1) >= 0)

    def down_exists(d):
        return jnp.logical_and(ia - 1 >= 0, ia + (d - 1) < n)

    def c_step(d):
        @pl.when(ia - d >= 0)
        def _():
            c_up(d).wait_recv()
            if d + 1 < n:
                @pl.when(ia + 1 < n)
                def _():
                    c_up(d + 1).start()
            c_pair_up(d).start()

        @pl.when(ia + d < n)
        def _():
            c_down(d).wait_recv()
            if d + 1 < n:
                @pl.when(ia - 1 >= 0)
                def _():
                    c_down(d + 1).start()
            c_pair_down(d).start()

    w_copy = pltpu.make_async_copy(w_hbm, w, loc.at[0])
    own_x = pltpu.make_async_copy(
        att.at[pl.ds(pl.multiple_of(ka * quart, quart), quart)], a_x.at[ka], loc.at[1])
    own_c = pltpu.make_async_copy(cot, c_g.at[ja, span(ia)], loc.at[2])
    own_a = pltpu.make_async_copy(a_x.at[ia], a_g.at[piece(ia, ka)], loc.at[3])
    for r in range(1, n):
        a_plane(r).start()
    own_x.start()

    @pl.when(up_exists(1))
    def _():
        c_up(1).start()

    @pl.when(down_exists(1))
    def _():
        c_down(1).start()

    c_pair_own.start()
    own_c.start()
    w_copy.start()
    own_x.wait()
    for r in range(1, n):
        a_plane(r).wait_recv()
    for r in range(1, n):
        a_z(r).start()
    own_a.start()
    own_a.wait()
    for r in range(1, n):
        a_spread(0, r).start()
    c_step(1)
    for b in range(1, n):
        a_z(b).wait_recv()
        for r in range(1, n):
            a_spread(b, r).start()
    for d in range(2, n - 1):
        c_step(d)
    for b in range(n):
        for r in range(1, n):
            a_spread(b, r).wait_recv()
    w_copy.wait()

    width = 256

    def project(which, out):
        @pl.loop(0, half // width)
        def _(c):
            at = pl.multiple_of(which * half + c * width, width)
            to = pl.multiple_of(c * width, width)
            out[:, pl.ds(to, width)] = jnp.dot(
                a_g[...], w[:, pl.ds(at, width)], preferred_element_type=f32
            ).astype(out.dtype)

    def pair(t):
        return remote(p_send.at[pl.ds(t * tok, tok)], p_recv.at[pl.ds(t * tok, tok)],
                      sp.at[t], rp.at[t], {"ja": other})

    project(other, p_send)
    for t in range(n):
        pair(t).start()
    project(ja, p_own)
    for t in range(n):
        pair(t).wait_recv()

    step_rows = 32

    def add_block(d, out, *incoming):
        @pl.loop(0, tok // step_rows)
        def _(i):
            at = pl.multiple_of(i * step_rows, step_rows)
            mine = pl.ds(d * tok + at, step_rows)
            here = pl.ds(at, step_rows)
            total = p_own[mine, :] + p_recv[mine, :].astype(f32)
            for ref in incoming:
                total = total + ref[here, :].astype(f32)
            out[here, :] = total.astype(bf16)

    def r_up(d):
        return remote(z_buf.at[d], z_up.at[d], sru.at[d], rru.at[d], {"ia": ia + 1})

    def r_down(d):
        return remote(z_buf.at[d], z_dn.at[d], srd.at[d], rrd.at[d], {"ia": ia - 1})

    def reduce_step(tau):
        for m in range(n):
            @pl.when(ia == m)
            def _():
                d = n - 1 - (tau - m)
                if 0 <= tau - m and d > m:
                    if m > 0:
                        r_up(d).wait_recv()
                        add_block(d, z_buf.at[d], z_up.at[d])
                    else:
                        add_block(d, z_buf.at[d])
                    r_up(d).start()
                d = tau - (n - 1 - m)
                if 0 <= d < m:
                    if m < n - 1:
                        r_down(d).wait_recv()
                        add_block(d, z_buf.at[d], z_dn.at[d])
                    else:
                        add_block(d, z_buf.at[d])
                    r_down(d).start()

    reduce_step(0)

    c_step(n - 1)
    own_c.wait()
    c_pair_own.wait_recv()
    for d in range(1, n):
        @pl.when(ia - d >= 0)
        def _():
            c_pair_up(d).wait_recv()

        @pl.when(ia + d < n)
        def _():
            c_pair_down(d).wait_recv()

    @pl.loop(0, rows_w // width)
    def _(c):
        at = pl.multiple_of(c * width, width)
        total = lax.dot_general(
            c_g[0], w[pl.ds(at, width), :half], (((1,), (1,)), ((), ())),
            preferred_element_type=f32)
        total = total + lax.dot_general(
            c_g[1], w[pl.ds(at, width), half:], (((1,), (1,)), ((), ())),
            preferred_element_type=f32)
        i_part[:, pl.ds(at, width)] = total.astype(bf16)

    def i_plane(b, r):
        q = plus(ka, r)
        t = plus(ia, b)
        return remote(i_part.at[piece(t, q)], i_recv.at[b, r - 1],
                      si.at[b, r - 1], ri.at[b, r - 1], {"ka": q})

    def i_to_z(b):
        return remote(i_red.at[b], i_z.at[ia], sz.at[b - 1], rz.at[b - 1], {"ia": plus(ia, b)})

    def i_back(r):
        k = plus(ka, r)
        return remote(i_z.at[k], i_out.at[pl.ds(pl.multiple_of(ka * quart, quart), quart)],
                      so.at[r - 1], ro.at[r - 1], {"ka": k})

    order = list(range(1, n)) + [0]
    for b in order:
        for r in range(1, n):
            i_plane(b, r).start()

    chunks = head // width

    def weight_chunks(first, last):
        @pl.loop(first, last)
        def _(c):
            at = pl.multiple_of(c * width, width)
            lhs = a_g[:, pl.ds(at, width)]
            for j in range(2):
                wg[pl.ds(at, width), j * half:(j + 1) * half] = lax.dot_general(
                    lhs, c_g[j], (((0,), (0,)), ((), ())), preferred_element_type=f32
                ).astype(bf16)

    weight_chunks(0, chunks // 2)
    reduce_step(1)
    for b in order:
        for r in range(1, n):
            i_plane(b, r).wait_recv()
        total = i_part[piece(plus(ia, b), ka), :].astype(f32)
        for r in range(1, n):
            total = total + i_recv[b, r - 1].astype(f32)
        if b == 0:
            i_z[ia] = total.astype(bf16)
        else:
            i_red[b] = total.astype(bf16)
            i_to_z(b).start()
    for tau in range(2, n - 1):
        reduce_step(tau)
    weight_chunks(chunks // 2, chunks)
    for b in range(1, n):
        i_to_z(b).wait_recv()
    for r in range(1, n):
        i_back(r).start()
    ig[pl.ds(pl.multiple_of(ka * quart, quart), quart), :] = i_z[ka]
    for m in range(n):
        @pl.when(ia == m)
        def _():
            incoming = []
            if m > 0:
                r_up(m).wait_recv()
                incoming.append(z_up.at[m])
            if m < n - 1:
                r_down(m).wait_recv()
                incoming.append(z_dn.at[m])
            add_block(m, proj, *incoming)
    for r in range(1, n):
        i_back(r).wait_recv()
        rows = pl.ds(pl.multiple_of(minus(ka, r) * quart, quart), quart)
        ig[rows, :] = i_out[rows, :]

    for r in range(1, n):
        a_plane(r).wait_send()
        a_z(r).wait_send()
        i_to_z(r).wait_send()
        i_back(r).wait_send()
        for b in range(n):
            a_spread(b, r).wait_send()
            i_plane(b, r).wait_send()
    c_pair_own.wait_send()
    for t in range(n):
        pair(t).wait_send()
    for d in range(1, n):
        @pl.when(up_exists(d))
        def _():
            c_up(d).wait_send()

        @pl.when(down_exists(d))
        def _():
            c_down(d).wait_send()

        @pl.when(ia - d >= 0)
        def _():
            c_pair_up(d).wait_send()

        @pl.when(ia + d < n)
        def _():
            c_pair_down(d).wait_send()

    for d in range(n):
        @pl.when(ia < d)
        def _():
            r_up(d).wait_send()

        @pl.when(ia > d)
        def _():
            r_down(d).wait_send()


def stationary_weight(n, attended, out_weight, cotangent):
    tok, head = attended.shape
    half = cotangent.shape[1]
    rows = n * tok
    quart = tok // n
    bf16, f32 = jnp.bfloat16, jnp.float32
    vmem = pl.BlockSpec(memory_space=pltpu.VMEM)
    dma = pltpu.SemaphoreType.DMA
    one = dma((n - 1,))
    two = dma((n, n - 1))
    full = dma((n,))
    flops = 6 * rows * out_weight.shape[0] * out_weight.shape[1]
    return pl.pallas_call(
        functools.partial(kernel, n),
        out_shape=(
            jax.ShapeDtypeStruct((tok, half), bf16),
            jax.ShapeDtypeStruct((tok, head), bf16),
            jax.ShapeDtypeStruct(out_weight.shape, bf16),
        ),
        in_specs=[vmem, pl.BlockSpec(memory_space=pl.ANY), vmem],
        out_specs=(vmem, vmem, vmem),
        scratch_shapes=[
            pltpu.VMEM(out_weight.shape, bf16),
            pltpu.VMEM((n, quart, head), bf16),
            pltpu.VMEM((rows, head), bf16),
            pltpu.VMEM((2, rows, half), bf16),
            pltpu.VMEM((rows, half), bf16),
            pltpu.VMEM((rows, half), bf16),
            pltpu.VMEM((rows, half), f32),
            pltpu.VMEM((n, tok, half), bf16),
            pltpu.VMEM((n, tok, half), bf16),
            pltpu.VMEM((n, tok, half), bf16),
            pltpu.VMEM((rows, head), bf16),
            pltpu.VMEM((n, n - 1, quart, head), bf16),
            pltpu.VMEM((n, quart, head), bf16),
            pltpu.VMEM((n, quart, head), bf16),
            pltpu.VMEM((tok, head), bf16),
            full, one, one, one, one, two, two, one, one, one, one,
            one, one, one, one, dma((1,)), dma((1,)),
            full, full, full, full, full, full, two, two, one, one, one, one,
        ],
        compiler_params=pltpu.CompilerParams(
            collective_id=0, has_side_effects=True, vmem_limit_bytes=VMEM_LIMIT
        ),
        cost_estimate=pl.CostEstimate(
            flops=flops, bytes_accessed=6 * rows * half, transcendentals=0
        ),
    )(attended, out_weight, cotangent)


def on_device(sizes, attended, out_weight, cotangent):
    tok, head = attended.shape
    half = cotangent.shape[1]
    n = sizes["ia"]
    tiles = tok % (16 * n) == 0 and head % 256 == 0 and half % 256 == 0
    fits = (
        sizes["ja"] == 2
        and sizes["ka"] == n
        and n >= 3
        and out_weight.shape == (head, 2 * half)
        and head % 512 == 0
        and 8 * out_weight.size + 2 * n * tok * (6 * head + 9 * half) < VMEM_LIMIT
    )
    if tiles and fits:
        return stationary_weight(n, attended, out_weight, cotangent)
    return gathered_weight(attended, out_weight, cotangent)


def solution(mesh):
    return jax.shard_map(
        functools.partial(on_device, dict(mesh.shape)),
        mesh=mesh,
        in_specs=(P("ia", ("ja", "ka")), P(("ja", "ia"), "ka"), P("ia", ("ka", "ja"))),
        out_specs=(P("ia", ("ka", "ja")), P("ia", ("ja", "ka")), P(("ja", "ia"), "ka")),
        check_vma=False,
    )
```

time: 685 us -> 111 us (0.16)
  waiting for transfers between devices: 637 us -> 0 us
  Pallas kernels: 0 us -> 101 us
  matrix products: 32.1 us -> 0 us
  between operations: 14.1 us -> 0.64 us
  local copies, waits for them, and re-layouts: 0.01 us -> 8.52 us
    all_gather x3 -> x0, waiting for transfers between devices: 322 us -> none  [the longest x1 285 us: on_device(): weight_local = lax.all_gather(out_weight, 'ia', axis=0, tiled=True)]
    reduce_scatter x3 -> x0, waiting for transfers between devices: 313 us -> none  [the longest x1 282 us: on_device(): lax.psum_scatter(weight_terms.astype(jnp.bfloat16), 'ia', scatter_dimensi...]
    pallas_call x0 -> x1, Pallas kernels: none -> 101 us  [stationary_weight(): pl.pallas_call(functools.partial(kernel, n), out_shape=(jax.ShapeDtypeStr...]
    dot_general x3 -> x0, matrix products: 32.1 us -> none  [the longest x1 12.1 us: on_device(): lax.dot_general(grad_rows, weight_local, (((1,), (1,)), ((), ())), prefer...]
    unnamed x4 -> x3, local copies, waits for them, and re-layouts: 0.01 us -> 8.52 us
  transfers between devices with their start and end apart: 6 -> 0, of which waited for: 5 -> 0; matrix products, arithmetic and copies ran while one was open for 5% -> 0% of each run, Pallas kernels for 0% -> 0%
where the time goes in v1:
time: 111 us; the launch traced here: 110 us
  Pallas kernels  101 us (91%)
  local copies, waits for them, and re-layouts  8.52 us (8%)
    pallas_call x1, Pallas kernels, stationary_weight(): pl.pallas_call(functools.partial(kernel, n), out_shape=(jax.ShapeDtypeStr...  101 us
    unnamed x3, local copies, waits for them, and re-layouts  8.52 us

profile of v1, /device:TPU:8, one launch (start us, length us, event | category | flops | bytes accessed | tf_op | source)
XLA Modules:
  0.0 110.0 jit_solution(15398144047610416165)
XLA Ops:
  0.6 100.8 %shard_map.58 = (bf16[256,1024]{1,0:T(8,128)(2,1)}, bf16[256,1024]{1,0:T(8,128)(2,1)}, bf16[1024,2048]{1,0:T(8,128)(2,1)}) custom-call(bf16[256,1024]{1,0:T(8,128)(2,1)} %att.1, bf16[1024,2048]{1,0:T(8,128)(2,1)} %w_hbm.1, bf16[256,1024]{1,0:T(8,128)(2,1)} %cot.1), custom_call_target="tpu_custom_call" | custom-call | flops 12884901888 | bytes 6291456 | tf_op jit(solution)/shard_map/pallas_call | solution.py:381
  101.5 1.9 %copy.9 = bf16[256,1024]{1,0:T(8,128)(2,1)} copy(bf16[256,1024]{1,0:T(8,128)(2,1)} %get-tuple-element.6) | data formatting | bytes 1048576
  103.3 1.9 %copy.10 = bf16[256,1024]{1,0:T(8,128)(2,1)} copy(bf16[256,1024]{1,0:T(8,128)(2,1)} %get-tuple-element.7) | data formatting | bytes 1048576
  105.2 4.8 %copy.11 = bf16[1024,2048]{1,0:T(8,128)(2,1)} copy(bf16[1024,2048]{1,0:T(8,128)(2,1)} %get-tuple-element.8) | data formatting | bytes 8388608

commit v2 on v1

--- a/solution.py
+++ b/solution.py
@@ -8,7 +8,7 @@
 from jax.sharding import PartitionSpec as P
 
 MESH = pl.DeviceIdType.MESH
-VMEM_LIMIT = 60 * 1024 * 1024
+VMEM_LIMIT = 44 * 1024 * 1024
 
 
 def gathered_weight(attended, out_weight, cotangent):
@@ -141,14 +141,6 @@
         a_plane(r).start()
     own_x.start()
 
-    @pl.when(up_exists(1))
-    def _():
-        c_up(1).start()
-
-    @pl.when(down_exists(1))
-    def _():
-        c_down(1).start()
-
     c_pair_own.start()
     own_c.start()
     w_copy.start()
@@ -157,23 +149,72 @@
         a_plane(r).wait_recv()
     for r in range(1, n):
         a_z(r).start()
+
+    @pl.when(up_exists(1))
+    def _():
+        c_up(1).start()
+
+    @pl.when(down_exists(1))
+    def _():
+        c_down(1).start()
+
     own_a.start()
     own_a.wait()
     for r in range(1, n):
         a_spread(0, r).start()
-    c_step(1)
+
+    width = 256
+
+    def i_plane(b, r):
+        q = plus(ka, r)
+        t = plus(ia, b)
+        return remote(i_part.at[piece(t, q)], i_recv.at[b, r - 1],
+                      si.at[b, r - 1], ri.at[b, r - 1], {"ka": q})
+
+    def input_block(t):
+        @pl.loop(0, rows_w // width)
+        def _(c):
+            at = pl.multiple_of(c * width, width)
+            total = lax.dot_general(
+                c_g[0, span(t), :], w[pl.ds(at, width), :half], (((1,), (1,)), ((), ())),
+                preferred_element_type=f32)
+            total = total + lax.dot_general(
+                c_g[1, span(t), :], w[pl.ds(at, width), half:], (((1,), (1,)), ((), ())),
+                preferred_element_type=f32)
+            i_part[span(t), pl.ds(at, width)] = total.astype(bf16)
+
+    def input_send(b):
+        for r in range(1, n):
+            i_plane(b, r).start()
+
+    def input_step(d):
+        @pl.when(ia - d >= 0)
+        def _():
+            c_pair_up(d).wait_recv()
+            input_block(ia - d)
+            input_send(n - d)
+
+        @pl.when(ia + d < n)
+        def _():
+            c_pair_down(d).wait_recv()
+            input_block(ia + d)
+            input_send(d)
+
+    w_copy.wait()
+    own_c.wait()
+    c_pair_own.wait_recv()
+    input_block(ia)
     for b in range(1, n):
         a_z(b).wait_recv()
         for r in range(1, n):
             a_spread(b, r).start()
-    for d in range(2, n - 1):
-        c_step(d)
+    input_send(0)
+    c_step(1)
+    input_step(1)
     for b in range(n):
         for r in range(1, n):
             a_spread(b, r).wait_recv()
-    w_copy.wait()
-
-    width = 256
+
 
     def project(which, out):
         @pl.loop(0, half // width)
@@ -191,6 +232,8 @@
     project(other, p_send)
     for t in range(n):
         pair(t).start()
+    for d in range(2, n - 1):
+        c_step(d)
     project(ja, p_own)
     for t in range(n):
         pair(t).wait_recv()
@@ -237,34 +280,10 @@
 
     reduce_step(0)
 
+    for d in range(2, n - 1):
+        input_step(d)
     c_step(n - 1)
-    own_c.wait()
-    c_pair_own.wait_recv()
-    for d in range(1, n):
-        @pl.when(ia - d >= 0)
-        def _():
-            c_pair_up(d).wait_recv()
-
-        @pl.when(ia + d < n)
-        def _():
-            c_pair_down(d).wait_recv()
-
-    @pl.loop(0, rows_w // width)
-    def _(c):
-        at = pl.multiple_of(c * width, width)
-        total = lax.dot_general(
-            c_g[0], w[pl.ds(at, width), :half], (((1,), (1,)), ((), ())),
-            preferred_element_type=f32)
-        total = total + lax.dot_general(
-            c_g[1], w[pl.ds(at, width), half:], (((1,), (1,)), ((), ())),
-            preferred_element_type=f32)
-        i_part[:, pl.ds(at, width)] = total.astype(bf16)
-
-    def i_plane(b, r):
-        q = plus(ka, r)
-        t = plus(ia, b)
-        return remote(i_part.at[piece(t, q)], i_recv.at[b, r - 1],
-                      si.at[b, r - 1], ri.at[b, r - 1], {"ka": q})
+    input_step(n - 1)
 
     def i_to_z(b):
         return remote(i_red.at[b], i_z.at[ia], sz.at[b - 1], rz.at[b - 1], {"ia": plus(ia, b)})
@@ -273,11 +292,6 @@
         k = plus(ka, r)
         return remote(i_z.at[k], i_out.at[pl.ds(pl.multiple_of(ka * quart, quart), quart)],
                       so.at[r - 1], ro.at[r - 1], {"ka": k})
-
-    order = list(range(1, n)) + [0]
-    for b in order:
-        for r in range(1, n):
-            i_plane(b, r).start()
 
     chunks = head // width
 
@@ -291,9 +305,9 @@
                     lhs, c_g[j], (((0,), (0,)), ((), ())), preferred_element_type=f32
                 ).astype(bf16)
 
+    reduce_step(1)
     weight_chunks(0, chunks // 2)
-    reduce_step(1)
-    for b in order:
+    for b in range(n):
         for r in range(1, n):
             i_plane(b, r).wait_recv()
         total = i_part[piece(plus(ia, b), ka), :].astype(f32)
@@ -427,7 +441,7 @@
         and n >= 3
         and out_weight.shape == (head, 2 * half)
         and head % 512 == 0
-        and 8 * out_weight.size + 2 * n * tok * (6 * head + 9 * half) < VMEM_LIMIT
+        and 4 * out_weight.size + 2 * n * tok * (5 * head + 10 * half) < VMEM_LIMIT
     )
     if tiles and fits:
         return stationary_weight(n, attended, out_weight, cotangent)

time: 111 us -> 103 us (0.928)
  Pallas kernels: 101 us -> 96.3 us
  local copies, waits for them, and re-layouts: 8.52 us -> 5.68 us
    pallas_call x1, Pallas kernels: 101 us -> 96.3 us  [stationary_weight(): pl.pallas_call(functools.partial(kernel, n), out_shape=(jax.ShapeDtypeStr...]
    unnamed x3 -> x7, local copies, waits for them, and re-layouts: 8.52 us -> 5.68 us
where the time goes in v2:
time: 103 us
  Pallas kernels  96.3 us (93%)
  local copies, waits for them, and re-layouts  5.68 us (6%)
    pallas_call x1, Pallas kernels, stationary_weight(): pl.pallas_call(functools.partial(kernel, n), out_shape=(jax.ShapeDtypeStr...  96.3 us
    unnamed x7, local copies, waits for them, and re-layouts  5.68 us

profile of v2, /device:TPU:8, one launch (start us, length us, event | category | flops | bytes accessed | tf_op | source)
XLA Modules:
  0.0 102.6 jit_solution(2017516217670666307)
XLA Ops:
  0.6 0.0 copy-start
  0.6 1.0 %copy-done = bf16[256,1024]{1,0:T(8,128)(2,1)S(1)} copy-done((bf16[256,1024]{1,0:T(8,128)(2,1)S(1)}, bf16[256,1024]{1,0:T(8,128)(2,1)}, u32[]{:S(2)}) %copy-start) | copy-done | bytes 524312
  1.7 0.0 copy-start.1
  1.7 1.0 %copy-done.1 = bf16[256,1024]{1,0:T(8,128)(2,1)S(1)} copy-done((bf16[256,1024]{1,0:T(8,128)(2,1)S(1)}, bf16[256,1024]{1,0:T(8,128)(2,1)}, u32[]{:S(2)}) %copy-start.1) | copy-done | bytes 524312
  2.7 96.3 %shard_map.58 = (bf16[256,1024]{1,0:T(8,128)(2,1)S(1)}, bf16[256,1024]{1,0:T(8,128)(2,1)S(1)}, bf16[1024,2048]{1,0:T(8,128)(2,1)S(1)}) custom-call(bf16[256,1024]{1,0:T(8,128)(2,1)S(1)} %copy-done, bf16[1024,2048]{1,0:T(8,128)(2,1)} %w_hbm.1, bf16[256,1024]{1,0:T(8,128)(2,1)S(1)} %copy-done.1), custom_call_target="tpu_custom_call" | custom-call | flops 12884901888 | bytes 6291456 | tf_op jit(solution)/shard_map/pallas_call | solution.py:395
  99.0 0.8 copy.9
  99.8 0.8 copy.10
  100.6 2.0 %copy.11 = bf16[1024,2048]{1,0:T(8,128)(2,1)} copy(bf16[1024,2048]{1,0:T(8,128)(2,1)S(1)} %get-tuple-element.8) | data formatting | bytes 8388608
Async XLA Ops:
  0.6 1.0 %copy-start = (bf16[256,1024]{1,0:T(8,128)(2,1)S(1)}, bf16[256,1024]{1,0:T(8,128)(2,1)}, u32[]{:S(2)}) copy-start(bf16[256,1024]{1,0:T(8,128)(2,1)} %att.1) | copy-start | bytes 1572868
  1.7 1.0 %copy-start.1 = (bf16[256,1024]{1,0:T(8,128)(2,1)S(1)}, bf16[256,1024]{1,0:T(8,128)(2,1)}, u32[]{:S(2)}) copy-start(bf16[256,1024]{1,0:T(8,128)(2,1)} %cot.1) | copy-start | bytes 1572868

commit v3 on v2

--- a/solution.py
+++ b/solution.py
@@ -261,21 +261,23 @@
         for m in range(n):
             @pl.when(ia == m)
             def _():
+                if m == 0 and tau == 0:
+                    for d in range(n - 1, 0, -1):
+                        add_block(d, z_buf.at[d])
+                        r_up(d).start()
                 d = n - 1 - (tau - m)
-                if 0 <= tau - m and d > m:
-                    if m > 0:
-                        r_up(d).wait_recv()
-                        add_block(d, z_buf.at[d], z_up.at[d])
-                    else:
+                if m > 0 and tau >= m and d > m:
+                    r_up(d).wait_recv()
+                    add_block(d, z_buf.at[d], z_up.at[d])
+                    r_up(d).start()
+                if m == n - 1 and tau == 0:
+                    for d in range(n - 1):
                         add_block(d, z_buf.at[d])
-                    r_up(d).start()
+                        r_down(d).start()
                 d = tau - (n - 1 - m)
-                if 0 <= d < m:
-                    if m < n - 1:
-                        r_down(d).wait_recv()
-                        add_block(d, z_buf.at[d], z_dn.at[d])
-                    else:
-                        add_block(d, z_buf.at[d])
+                if m < n - 1 and 0 <= d < m:
+                    r_down(d).wait_recv()
+                    add_block(d, z_buf.at[d], z_dn.at[d])
                     r_down(d).start()
 
     reduce_step(0)

time: 103 us -> 104 us (level)
  no operation moved by 1% of the time
where the time goes in v3:
time: 104 us; the launch traced here: 103 us
  Pallas kernels  96.3 us (93%)
  local copies, waits for them, and re-layouts  5.68 us (5%)
    pallas_call x1, Pallas kernels, stationary_weight(): pl.pallas_call(functools.partial(kernel, n), out_shape=(jax.ShapeDtypeStr...  96.3 us
    unnamed x7, local copies, waits for them, and re-layouts  5.68 us

profile of v3, /device:TPU:8, one launch (start us, length us, event | category | flops | bytes accessed | tf_op | source)
XLA Modules:
  0.0 102.6 jit_solution(729480568106343240)
XLA Ops:
  0.6 0.0 copy-start
  0.6 1.0 %copy-done = bf16[256,1024]{1,0:T(8,128)(2,1)S(1)} copy-done((bf16[256,1024]{1,0:T(8,128)(2,1)S(1)}, bf16[256,1024]{1,0:T(8,128)(2,1)}, u32[]{:S(2)}) %copy-start) | copy-done | bytes 524312
  1.7 0.0 copy-start.1
  1.7 1.0 %copy-done.1 = bf16[256,1024]{1,0:T(8,128)(2,1)S(1)} copy-done((bf16[256,1024]{1,0:T(8,128)(2,1)S(1)}, bf16[256,1024]{1,0:T(8,128)(2,1)}, u32[]{:S(2)}) %copy-start.1) | copy-done | bytes 524312
  2.7 96.3 %shard_map.58 = (bf16[256,1024]{1,0:T(8,128)(2,1)S(1)}, bf16[256,1024]{1,0:T(8,128)(2,1)S(1)}, bf16[1024,2048]{1,0:T(8,128)(2,1)S(1)}) custom-call(bf16[256,1024]{1,0:T(8,128)(2,1)S(1)} %copy-done, bf16[1024,2048]{1,0:T(8,128)(2,1)} %w_hbm.1, bf16[256,1024]{1,0:T(8,128)(2,1)S(1)} %copy-done.1), custom_call_target="tpu_custom_call" | custom-call | flops 12884901888 | bytes 6291456 | tf_op jit(solution)/shard_map/pallas_call | solution.py:397
  99.0 0.8 copy.9
  99.8 0.8 copy.10
  100.6 2.0 %copy.11 = bf16[1024,2048]{1,0:T(8,128)(2,1)} copy(bf16[1024,2048]{1,0:T(8,128)(2,1)S(1)} %get-tuple-element.8) | data formatting | bytes 8388608
Async XLA Ops:
  0.6 1.0 %copy-start = (bf16[256,1024]{1,0:T(8,128)(2,1)S(1)}, bf16[256,1024]{1,0:T(8,128)(2,1)}, u32[]{:S(2)}) copy-start(bf16[256,1024]{1,0:T(8,128)(2,1)} %att.1) | copy-start | bytes 1572868
  1.7 1.0 %copy-start.1 = (bf16[256,1024]{1,0:T(8,128)(2,1)S(1)}, bf16[256,1024]{1,0:T(8,128)(2,1)}, u32[]{:S(2)}) copy-start(bf16[256,1024]{1,0:T(8,128)(2,1)} %cot.1) | copy-start | bytes 1572868
